TPU v7x, 32 devices: a whole 2x2x4 slice. The times are simulated.
32 devices in a mesh: tm: 4 (over y, x), space: 8 (over z, core).
Axes of the slice: x: 2, y: 2, z: 4, core: 2. Of those that a mesh axis runs over, the one named last changes fastest.
Arguments:
- positions: float32 [4, 3, 3, 2048], P('tm', None, None, 'space'), may hold values from -4 to 4
- velocities: float32 [4, 3, 3, 2048], P('tm', None, None, 'space'), may hold values from -3 to 3
- masses: float32 [2048], P('space'), may hold values from 0.2 to 2
- initial_places: float32 [3, 2048], P(None, 'space'), may hold values from -4 to 4
- initial_speeds: float32 [3, 2048], P(None, 'space'), may hold values from -3 to 3
Outputs:
- node_places: float32 [4, 2, 3, 2048], P('tm', None, None, 'space')
- node_speeds: float32 [4, 2, 3, 2048], P('tm', None, None, 'space')
- end_force: float32 [4, 3, 2048], P('tm', None, 'space')
- start_places: float32 [4, 3, 2048], P('tm', None, 'space')
- start_speeds: float32 [4, 3, 2048], P('tm', None, 'space')
All inputs are finite; a program needn't handle non-finite values.
Results may differ from a plain program's by a relative error of at most 0.0003.
Values sent between devices are 32-bit elements; how exact they have to be, the bound alone decides.
A program may use at most 64 MiB of HBM per device.

v0:
```python
import jax
import jax.numpy as jnp
from jax import lax
from jax.sharding import PartitionSpec as P

soften = 0.01
slice_length = 0.25
lobatto_weights = ((5.0 / 24.0, 1.0 / 3.0, -1.0 / 24.0), (-1.0 / 24.0, 1.0 / 3.0, 5.0 / 24.0))


def passed_along(value, axis, steps):
    count = lax.axis_size(axis)
    pairs = [(source, (source + steps) % count) for source in range(count)]
    return lax.ppermute(value, axis, pairs)


def entering(value, axis, join, neutral):
    count, mine = (lax.axis_size(axis), lax.axis_index(axis))
    pieces = jax.tree.map(lambda part: lax.all_gather(part, axis), value)
    so_far = jax.tree.map(
        lambda part, zero: jnp.full_like(part, 0) + jnp.asarray(zero, part.dtype), value, neutral
    )

    def step(position, so_far):
        longer = join(so_far, jax.tree.map(lambda part: part[position], pieces))
        return jax.tree.map(lambda new, old: jnp.where(position < mine, new, old), longer, so_far)

    return lax.fori_loop(0, count - 1, step, so_far)


def pair_kernel(local_places, remote_places):
    squared = (remote_places[:, 0, None, :] - local_places[:, 0, :, None]) ** 2
    squared = squared + (remote_places[:, 1, None, :] - local_places[:, 1, :, None]) ** 2
    squared = squared + (remote_places[:, 2, None, :] - local_places[:, 2, :, None]) ** 2
    inverse = lax.rsqrt(squared + soften)
    return inverse * inverse * inverse


def attract(kernel, local_places, remote_places, remote_mass):
    weighted = remote_places * remote_mass
    summed = jnp.einsum("nij,ncj->nci", kernel, weighted, precision=lax.Precision.HIGHEST)
    kernel_sum = jnp.einsum(
        "nij,nj->ni", kernel, remote_mass[:, 0], precision=lax.Precision.HIGHEST
    )
    return summed - local_places * kernel_sum[:, None, :]


def reaction(kernel, local_places, local_mass, remote_places):
    weighted = local_places * local_mass
    summed = jnp.einsum("nij,nci->ncj", kernel, weighted, precision=lax.Precision.HIGHEST)
    kernel_sum = jnp.einsum("nij,ni->nj", kernel, local_mass[:, 0], precision=lax.Precision.HIGHEST)
    return summed - remote_places * kernel_sum[:, None, :]


def gravity(places, masses):
    cycle_size = lax.axis_size("space")
    body_count = places.shape[2] * cycle_size
    mass_cube = jnp.broadcast_to(masses[None, None, :], (places.shape[0], 1, places.shape[2]))
    halfway = cycle_size // 2
    own_force = attract(pair_kernel(places, places), places, places, mass_cube)

    def cycle_turn(stride, carry):
        force, travel = carry
        moved_places, moved_mass, moved_react = passed_along(
            (travel[0], travel[1], travel[2]), "space", 1
        )
        kernel = pair_kernel(places, moved_places)
        force = force + attract(kernel, places, moved_places, moved_mass)
        weight_on = jnp.where(stride < halfway, 1.0, 0.0).astype(jnp.float32)
        moved_react = moved_react + weight_on * reaction(kernel, places, mass_cube, moved_places)
        return (force, (moved_places, moved_mass, moved_react))

    force, travel = lax.fori_loop(
        1, halfway + 1, cycle_turn, (own_force, (places, mass_cube, jnp.zeros_like(places)))
    )
    returned = passed_along(travel[2], "space", -halfway)
    return (force + returned) / body_count


def body(positions, velocities, masses, initial_places, initial_speeds):
    places = positions[0]
    speeds = velocities[0]
    stacked = gravity(places, masses)
    earlier = [stacked[0], stacked[1], stacked[2]]
    new_places = [places[0]]
    new_speeds = [speeds[0]]
    new_force = [earlier[0]]
    half_step = 0.5 * slice_length
    for node in range(2):
        weights = lobatto_weights[node]
        moved = slice_length * (
            weights[0] * speeds[0] + weights[1] * speeds[1] + weights[2] * speeds[2]
        )
        kicked = slice_length * (
            weights[0] * earlier[0] + weights[1] * earlier[1] + weights[2] * earlier[2]
        )
        place = new_places[node] + half_step * (new_speeds[node] - speeds[node]) + moved
        speed = new_speeds[node] + half_step * (new_force[node] - earlier[node]) + kicked
        new_places.append(place)
        new_speeds.append(speed)
        new_force.append(gravity(place[None], masses)[0])
    drift_place = new_places[2] - (places[0] + slice_length * speeds[0])
    drift_speed = new_speeds[2] - speeds[0]

    def combine(earlier_part, latter_part):
        return (
            earlier_part[0] + latter_part[2] * slice_length * earlier_part[1] + latter_part[0],
            earlier_part[1] + latter_part[1],
            earlier_part[2] + latter_part[2],
        )

    nothing = jnp.zeros_like(drift_place)
    prefix = entering(
        (drift_place, drift_speed, jnp.ones((), jnp.float32)),
        "tm",
        combine,
        (nothing, nothing, jnp.zeros((), jnp.float32)),
    )
    slice_index = lax.axis_index("tm").astype(jnp.float32)
    start_place = initial_places + slice_index * slice_length * initial_speeds + prefix[0]
    start_speed = initial_speeds + prefix[1]
    return (
        jnp.stack(new_places[1:])[None],
        jnp.stack(new_speeds[1:])[None],
        new_force[2][None],
        start_place[None],
        start_speed[None],
    )


def solution(mesh):
    return jax.shard_map(
        body,
        mesh=mesh,
        in_specs=(
            P("tm", None, None, "space"),
            P("tm", None, None, "space"),
            P("space"),
            P(None, "space"),
            P(None, "space"),
        ),
        out_specs=(
            P("tm", None, None, "space"),
            P("tm", None, None, "space"),
            P("tm", None, "space"),
            P("tm", None, "space"),
            P("tm", None, "space"),
        ),
        check_vma=False,
    )
```

profile of v0, /device:TPU:0, one launch (start us, length us, event | category | flops | bytes accessed | tf_op | source)
XLA Modules:
  0.0 133.2 jit_solution(12158480183190474268)
XLA Ops:
  2.1 1.1 fusion.54
  3.2 1.1 convolution_subtract_fusion.3
  4.3 37.3 %while.76 = (s32[]{:T(128)}, f32[3,3,256]{2,1,0:T(4,128)S(1)}, f32[3,3,256]{2,1,0:T(4,128)S(1)}, f32[3,1,256]{2,0,1:T(4,128)S(1)}, f32[3,3,256]{2,1,0:T(4,128)S(...) while((s32[]{:T(128)}, f32[3,3,256]{2,1,0:T(4,128)S(1)}, ...), condition=%wide.region_1.2_spmd.clone, body=%wide.region_0.1_spmd.clone.sunk | while | flops 27548164 | bytes 383257 | solution.py:73
  4.8 2.7 %collective-permute-start.1 = (f32[3,1,256]{2,0,1:T(4,128)S(1)}, f32[3,1,256]{2,0,1:T(4,128)S(1)}, u32[]{:S(2)}, u32[]{:S(2)}) collective-permute-start(f32[3,1,256]{2,0,1:T(4,128)S(1)} %get-tuple-element.1037), channel_id=1, source_target_pairs={{0,1},{1,2},{2,3},{3,4},{4,5},{5,6},{6,7},{7,0},{8,9},{9,10},{10,1... | collective-permute-start | bytes 9224 | tf_op jit(solution)/shard_map/while/body/eval_jaxpr/ppermute | solution.py:14
  7.6 2.7 %collective-permute-done.1 = f32[3,1,256]{2,0,1:T(4,128)S(1)} collective-permute-done((f32[3,1,256]{2,0,1:T(4,128)S(1)}, f32[3,1,256]{2,0,1:T(4,128)S(1)}, u32[]{:S(2)}, u32[]{:S(2)}) %collective-permute-start.1) | collective-permute-done | bytes 3104 | tf_op jit(solution)/shard_map/while/body/eval_jaxpr/ppermute | solution.py:14
  10.3 1.1 fusion.208
  11.4 1.1 fusion.209
  12.5 0.9 fusion.210
  15.1 4.2 %collective-permute-done.1 = f32[3,1,256]{2,0,1:T(4,128)S(1)} collective-permute-done((f32[3,1,256]{2,0,1:T(4,128)S(1)}, f32[3,1,256]{2,0,1:T(4,128)S(1)}, u32[]{:S(2)}, u32[]{:S(2)}) %collective-permute-start.1) | collective-permute-done | bytes 3104 | tf_op jit(solution)/shard_map/while/body/eval_jaxpr/ppermute | solution.py:14
  19.4 1.1 fusion.208
  20.5 1.1 fusion.209
  23.7 4.7 %collective-permute-done.1 = f32[3,1,256]{2,0,1:T(4,128)S(1)} collective-permute-done((f32[3,1,256]{2,0,1:T(4,128)S(1)}, f32[3,1,256]{2,0,1:T(4,128)S(1)}, u32[]{:S(2)}, u32[]{:S(2)}) %collective-permute-start.1) | collective-permute-done | bytes 3104 | tf_op jit(solution)/shard_map/while/body/eval_jaxpr/ppermute | solution.py:14
  28.5 1.1 fusion.208
  29.6 1.1 fusion.209
  32.8 4.7 %collective-permute-done.1 = f32[3,1,256]{2,0,1:T(4,128)S(1)} collective-permute-done((f32[3,1,256]{2,0,1:T(4,128)S(1)}, f32[3,1,256]{2,0,1:T(4,128)S(1)}, u32[]{:S(2)}, u32[]{:S(2)}) %collective-permute-start.1) | collective-permute-done | bytes 3104 | tf_op jit(solution)/shard_map/while/body/eval_jaxpr/ppermute | solution.py:14
  37.6 1.1 fusion.208
  38.7 1.1 fusion.209
  45.3 27.0 %while.77 = (s32[]{:T(128)}, f32[1,3,256]{2,1,0:T(4,128)S(1)}, f32[1,3,256]{2,1,0:T(4,128)S(1)}, f32[1,1,256]{2,1,0:T(1,128)S(1)}, f32[1,3,256]{2,1,0:T(4,128)S(...) while((s32[]{:T(128)}, f32[1,3,256]{2,1,0:T(4,128)S(1)}, ...), condition=%wide.region_3.4_spmd.clone, body=%wide.region_2.3_spmd.clone.sunk | while | flops 9182725 | bytes 112921 | solution.py:73
  45.5 4.7 %collective-permute-done.4 = f32[1,1,256]{2,1,0:T(1,128)S(1)} collective-permute-done((f32[1,1,256]{2,1,0:T(1,128)S(1)}, f32[1,1,256]{2,1,0:T(1,128)S(1)}, u32[]{:S(2)}, u32[]{:S(2)}) %collective-permute-start.4) | collective-permute-done | bytes 1056 | tf_op jit(solution)/shard_map/while/body/eval_jaxpr/ppermute | solution.py:14
  52.3 4.7 %collective-permute-done.4 = f32[1,1,256]{2,1,0:T(1,128)S(1)} collective-permute-done((f32[1,1,256]{2,1,0:T(1,128)S(1)}, f32[1,1,256]{2,1,0:T(1,128)S(1)}, u32[]{:S(2)}, u32[]{:S(2)}) %collective-permute-start.4) | collective-permute-done | bytes 1056 | tf_op jit(solution)/shard_map/while/body/eval_jaxpr/ppermute | solution.py:14
  59.0 4.7 %collective-permute-done.4 = f32[1,1,256]{2,1,0:T(1,128)S(1)} collective-permute-done((f32[1,1,256]{2,1,0:T(1,128)S(1)}, f32[1,1,256]{2,1,0:T(1,128)S(1)}, u32[]{:S(2)}, u32[]{:S(2)}) %collective-permute-start.4) | collective-permute-done | bytes 1056 | tf_op jit(solution)/shard_map/while/body/eval_jaxpr/ppermute | solution.py:14
  65.8 4.7 %collective-permute-done.4 = f32[1,1,256]{2,1,0:T(1,128)S(1)} collective-permute-done((f32[1,1,256]{2,1,0:T(1,128)S(1)}, f32[1,1,256]{2,1,0:T(1,128)S(1)}, u32[]{:S(2)}, u32[]{:S(2)}) %collective-permute-start.4) | collective-permute-done | bytes 1056 | tf_op jit(solution)/shard_map/while/body/eval_jaxpr/ppermute | solution.py:14
  72.4 10.4 %all-reduce = f32[4]{0:T(128)S(1)} all-reduce(f32[4]{0:T(128)S(1)} %dynamic-update-slice), channel_id=1, replica_groups=mesh['tm'=4,'space'=8] {'tm'}, use_global_device_ids=true, to_apply=%add | all-reduce | flops 4 | bytes 32
  83.9 27.0 %while.78 = (s32[]{:T(128)}, f32[1,3,256]{2,1,0:T(4,128)S(1)}, f32[1,3,256]{2,1,0:T(4,128)S(1)}, f32[1,1,256]{2,1,0:T(1,128)S(1)}, f32[1,3,256]{2,1,0:T(4,128)S(...) while((s32[]{:T(128)}, f32[1,3,256]{2,1,0:T(4,128)S(1)}, ...), condition=%wide.region_5.6_spmd.clone, body=%wide.region_4.5_spmd.clone.sunk | while | flops 9182725 | bytes 112921 | solution.py:73
  83.9 1.3 collective-permute-start.7
  85.3 3.5 %collective-permute-done.7 = f32[1,1,256]{2,1,0:T(1,128)S(1)} collective-permute-done((f32[1,1,256]{2,1,0:T(1,128)S(1)}, f32[1,1,256]{2,1,0:T(1,128)S(1)}, u32[]{:S(2)}, u32[]{:S(2)}) %collective-permute-start.7) | collective-permute-done | bytes 1056 | tf_op jit(solution)/shard_map/while/body/eval_jaxpr/ppermute | solution.py:14
  91.1 4.4 %collective-permute-done.7 = f32[1,1,256]{2,1,0:T(1,128)S(1)} collective-permute-done((f32[1,1,256]{2,1,0:T(1,128)S(1)}, f32[1,1,256]{2,1,0:T(1,128)S(1)}, u32[]{:S(2)}, u32[]{:S(2)}) %collective-permute-start.7) | collective-permute-done | bytes 1056 | tf_op jit(solution)/shard_map/while/body/eval_jaxpr/ppermute | solution.py:14
  97.6 4.7 %collective-permute-done.7 = f32[1,1,256]{2,1,0:T(1,128)S(1)} collective-permute-done((f32[1,1,256]{2,1,0:T(1,128)S(1)}, f32[1,1,256]{2,1,0:T(1,128)S(1)}, u32[]{:S(2)}, u32[]{:S(2)}) %collective-permute-start.7) | collective-permute-done | bytes 1056 | tf_op jit(solution)/shard_map/while/body/eval_jaxpr/ppermute | solution.py:14
  104.4 4.7 %collective-permute-done.7 = f32[1,1,256]{2,1,0:T(1,128)S(1)} collective-permute-done((f32[1,1,256]{2,1,0:T(1,128)S(1)}, f32[1,1,256]{2,1,0:T(1,128)S(1)}, u32[]{:S(2)}, u32[]{:S(2)}) %collective-permute-start.7) | collective-permute-done | bytes 1056 | tf_op jit(solution)/shard_map/while/body/eval_jaxpr/ppermute | solution.py:14
  111.0 7.2 %all_gather.12 = f32[4,3,256]{2,1,0:T(4,128)S(1)} all-gather(f32[1,3,256]{2,1,0:T(4,128)S(1)} %get-tuple-element.741), channel_id=1, replica_groups=mesh['tm'=4,'space'=8] {'tm'}, dimensions={0}, use_global_device_ids=true | all-gather | bytes 15360 | tf_op jit(solution)/shard_map/all_gather | solution.py:19
  118.2 8.1 %all_gather.13 = f32[4,3,256]{2,1,0:T(4,128)S(1)} all-gather(f32[1,3,256]{2,1,0:T(4,128)S(1)} %get-tuple-element.738), channel_id=1, replica_groups=mesh['tm'=4,'space'=8] {'tm'}, dimensions={0}, use_global_device_ids=true | all-gather | bytes 15360 | tf_op jit(solution)/shard_map/all_gather | solution.py:19
  126.3 3.8 %while.79 = (s32[]{:T(128)}, f32[3,256]{1,0:T(4,128)S(1)}, f32[3,256]{1,0:T(4,128)S(1)}, s32[]{:T(128)}, f32[4]{0:T(128)S(1)}, /*index=5*/f32[4,3,256]{2,1,0:T(4...) while((s32[]{:T(128)}, f32[3,256]{1,0:T(4,128)S(1)}, ...), condition=%wide.region_7.8_spmd.clone, body=%wide.region_6.7_spmd.clone.sunk | while | flops 6149 | bytes 18593 | solution.py:28
  (245 shorter events, 34.9 us)
Async XLA Ops:
  4.3 6.0 %collective-permute-start = (f32[3,3,256]{2,1,0:T(4,128)S(1)}, f32[3,3,256]{2,1,0:T(4,128)S(1)}, u32[]{:S(2)}, u32[]{:S(2)}) collective-permute-start(f32[3,3,256]{2,1,0:T(4,128)S(1)} %get-tuple-element.1036), channel_id=1, source_target_pairs={{0,1},{1,2},{2,3},{3,4},{4,5},{5,6},{6,7},{7,0},{8,9},{9,10},{10,1... | collective-permute-start | bytes 27656 | tf_op jit(solution)/shard_map/while/body/eval_jaxpr/ppermute | solution.py:14
  4.8 5.4 %collective-permute-start.1 = (f32[3,1,256]{2,0,1:T(4,128)S(1)}, f32[3,1,256]{2,0,1:T(4,128)S(1)}, u32[]{:S(2)}, u32[]{:S(2)}) collective-permute-start(f32[3,1,256]{2,0,1:T(4,128)S(1)} %get-tuple-element.1037), channel_id=1, source_target_pairs={{0,1},{1,2},{2,3},{3,4},{4,5},{5,6},{6,7},{7,0},{8,9},{9,10},{10,1... | collective-permute-start | bytes 9224 | tf_op jit(solution)/shard_map/while/body/eval_jaxpr/ppermute | solution.py:14
  7.5 6.0 %collective-permute-start.2 = (f32[3,3,256]{2,1,0:T(4,128)S(1)}, f32[3,3,256]{2,1,0:T(4,128)S(1)}, u32[]{:S(2)}, u32[]{:S(2)}) collective-permute-start(f32[3,3,256]{2,1,0:T(4,128)S(1)} %broadcast_select_fusion.6), channel_id=1, source_target_pairs={{0,1},{1,2},{2,3},{3,4},{4,5},{5,6},{6,7},{7,0},{8,9},{9,10},{10,1... | collective-permute-start | bytes 27656 | tf_op jit(solution)/shard_map/while/body/eval_jaxpr/ppermute | solution.py:14
  14.3 5.0 %collective-permute-start = (f32[3,3,256]{2,1,0:T(4,128)S(1)}, f32[3,3,256]{2,1,0:T(4,128)S(1)}, u32[]{:S(2)}, u32[]{:S(2)}) collective-permute-start(f32[3,3,256]{2,1,0:T(4,128)S(1)} %get-tuple-element.1036), channel_id=1, source_target_pairs={{0,1},{1,2},{2,3},{3,4},{4,5},{5,6},{6,7},{7,0},{8,9},{9,10},{10,1... | collective-permute-start | bytes 27656 | tf_op jit(solution)/shard_map/while/body/eval_jaxpr/ppermute | solution.py:14
  14.4 4.9 %collective-permute-start.1 = (f32[3,1,256]{2,0,1:T(4,128)S(1)}, f32[3,1,256]{2,0,1:T(4,128)S(1)}, u32[]{:S(2)}, u32[]{:S(2)}) collective-permute-start(f32[3,1,256]{2,0,1:T(4,128)S(1)} %get-tuple-element.1037), channel_id=1, source_target_pairs={{0,1},{1,2},{2,3},{3,4},{4,5},{5,6},{6,7},{7,0},{8,9},{9,10},{10,1... | collective-permute-start | bytes 9224 | tf_op jit(solution)/shard_map/while/body/eval_jaxpr/ppermute | solution.py:14
  14.8 7.8 %collective-permute-start.2 = (f32[3,3,256]{2,1,0:T(4,128)S(1)}, f32[3,3,256]{2,1,0:T(4,128)S(1)}, u32[]{:S(2)}, u32[]{:S(2)}) collective-permute-start(f32[3,3,256]{2,1,0:T(4,128)S(1)} %broadcast_select_fusion.6), channel_id=1, source_target_pairs={{0,1},{1,2},{2,3},{3,4},{4,5},{5,6},{6,7},{7,0},{8,9},{9,10},{10,1... | collective-permute-start | bytes 27656 | tf_op jit(solution)/shard_map/while/body/eval_jaxpr/ppermute | solution.py:14
  23.4 5.0 %collective-permute-start = (f32[3,3,256]{2,1,0:T(4,128)S(1)}, f32[3,3,256]{2,1,0:T(4,128)S(1)}, u32[]{:S(2)}, u32[]{:S(2)}) collective-permute-start(f32[3,3,256]{2,1,0:T(4,128)S(1)} %get-tuple-element.1036), channel_id=1, source_target_pairs={{0,1},{1,2},{2,3},{3,4},{4,5},{5,6},{6,7},{7,0},{8,9},{9,10},{10,1... | collective-permute-start | bytes 27656 | tf_op jit(solution)/shard_map/while/body/eval_jaxpr/ppermute | solution.py:14
  23.5 4.9 %collective-permute-start.1 = (f32[3,1,256]{2,0,1:T(4,128)S(1)}, f32[3,1,256]{2,0,1:T(4,128)S(1)}, u32[]{:S(2)}, u32[]{:S(2)}) collective-permute-start(f32[3,1,256]{2,0,1:T(4,128)S(1)} %get-tuple-element.1037), channel_id=1, source_target_pairs={{0,1},{1,2},{2,3},{3,4},{4,5},{5,6},{6,7},{7,0},{8,9},{9,10},{10,1... | collective-permute-start | bytes 9224 | tf_op jit(solution)/shard_map/while/body/eval_jaxpr/ppermute | solution.py:14
  23.6 8.1 %collective-permute-start.2 = (f32[3,3,256]{2,1,0:T(4,128)S(1)}, f32[3,3,256]{2,1,0:T(4,128)S(1)}, u32[]{:S(2)}, u32[]{:S(2)}) collective-permute-start(f32[3,3,256]{2,1,0:T(4,128)S(1)} %broadcast_select_fusion.6), channel_id=1, source_target_pairs={{0,1},{1,2},{2,3},{3,4},{4,5},{5,6},{6,7},{7,0},{8,9},{9,10},{10,1... | collective-permute-start | bytes 27656 | tf_op jit(solution)/shard_map/while/body/eval_jaxpr/ppermute | solution.py:14
  32.5 5.0 %collective-permute-start = (f32[3,3,256]{2,1,0:T(4,128)S(1)}, f32[3,3,256]{2,1,0:T(4,128)S(1)}, u32[]{:S(2)}, u32[]{:S(2)}) collective-permute-start(f32[3,3,256]{2,1,0:T(4,128)S(1)} %get-tuple-element.1036), channel_id=1, source_target_pairs={{0,1},{1,2},{2,3},{3,4},{4,5},{5,6},{6,7},{7,0},{8,9},{9,10},{10,1... | collective-permute-start | bytes 27656 | tf_op jit(solution)/shard_map/while/body/eval_jaxpr/ppermute | solution.py:14
  32.6 4.9 %collective-permute-start.1 = (f32[3,1,256]{2,0,1:T(4,128)S(1)}, f32[3,1,256]{2,0,1:T(4,128)S(1)}, u32[]{:S(2)}, u32[]{:S(2)}) collective-permute-start(f32[3,1,256]{2,0,1:T(4,128)S(1)} %get-tuple-element.1037), channel_id=1, source_target_pairs={{0,1},{1,2},{2,3},{3,4},{4,5},{5,6},{6,7},{7,0},{8,9},{9,10},{10,1... | collective-permute-start | bytes 9224 | tf_op jit(solution)/shard_map/while/body/eval_jaxpr/ppermute | solution.py:14
  32.7 8.1 %collective-permute-start.2 = (f32[3,3,256]{2,1,0:T(4,128)S(1)}, f32[3,3,256]{2,1,0:T(4,128)S(1)}, u32[]{:S(2)}, u32[]{:S(2)}) collective-permute-start(f32[3,3,256]{2,1,0:T(4,128)S(1)} %broadcast_select_fusion.6), channel_id=1, source_target_pairs={{0,1},{1,2},{2,3},{3,4},{4,5},{5,6},{6,7},{7,0},{8,9},{9,10},{10,1... | collective-permute-start | bytes 27656 | tf_op jit(solution)/shard_map/while/body/eval_jaxpr/ppermute | solution.py:14
  41.6 41.2 %collective-permute-start.9 = (f32[3,3,256]{2,1,0:T(4,128)S(1)}, f32[3,3,256]{2,1,0:T(4,128)S(1)}, u32[]{:S(2)}, u32[]{:S(2)}) collective-permute-start(f32[3,3,256]{2,1,0:T(4,128)S(1)} %get-tuple-element.551), channel_id=1, source_target_pairs={{0,4},{1,5},{2,6},{3,7},{4,0},{5,1},{6,2},{7,3},{8,12},{9,13},{10,... | collective-permute-start | bytes 27656 | tf_op jit(solution)/shard_map/ppermute | solution.py:14
  45.3 4.9 %collective-permute-start.3 = (f32[1,3,256]{2,1,0:T(4,128)S(1)}, f32[1,3,256]{2,1,0:T(4,128)S(1)}, u32[]{:S(2)}, u32[]{:S(2)}) collective-permute-start(f32[1,3,256]{2,1,0:T(4,128)S(1)} %get-tuple-element.1075), channel_id=1, source_target_pairs={{0,1},{1,2},{2,3},{3,4},{4,5},{5,6},{6,7},{7,0},{8,9},{9,10},{10,1... | collective-permute-start | bytes 9224 | tf_op jit(solution)/shard_map/while/body/eval_jaxpr/ppermute | solution.py:14
  45.4 4.9 %collective-permute-start.4 = (f32[1,1,256]{2,1,0:T(1,128)S(1)}, f32[1,1,256]{2,1,0:T(1,128)S(1)}, u32[]{:S(2)}, u32[]{:S(2)}) collective-permute-start(f32[1,1,256]{2,1,0:T(1,128)S(1)} %get-tuple-element.1076), channel_id=1, source_target_pairs={{0,1},{1,2},{2,3},{3,4},{4,5},{5,6},{6,7},{7,0},{8,9},{9,10},{10,1... | collective-permute-start | bytes 3080 | tf_op jit(solution)/shard_map/while/body/eval_jaxpr/ppermute | solution.py:14
  45.4 6.2 %collective-permute-start.5 = (f32[1,3,256]{2,1,0:T(4,128)S(1)}, f32[1,3,256]{2,1,0:T(4,128)S(1)}, u32[]{:S(2)}, u32[]{:S(2)}) collective-permute-start(f32[1,3,256]{2,1,0:T(4,128)S(1)} %broadcast_select_fusion.7), channel_id=1, source_target_pairs={{0,1},{1,2},{2,3},{3,4},{4,5},{5,6},{6,7},{7,0},{8,9},{9,10},{10,1... | collective-permute-start | bytes 9224 | tf_op jit(solution)/shard_map/while/body/eval_jaxpr/ppermute | solution.py:14
  52.0 5.0 %collective-permute-start.3 = (f32[1,3,256]{2,1,0:T(4,128)S(1)}, f32[1,3,256]{2,1,0:T(4,128)S(1)}, u32[]{:S(2)}, u32[]{:S(2)}) collective-permute-start(f32[1,3,256]{2,1,0:T(4,128)S(1)} %get-tuple-element.1075), channel_id=1, source_target_pairs={{0,1},{1,2},{2,3},{3,4},{4,5},{5,6},{6,7},{7,0},{8,9},{9,10},{10,1... | collective-permute-start | bytes 9224 | tf_op jit(solution)/shard_map/while/body/eval_jaxpr/ppermute | solution.py:14
  52.2 6.2 %collective-permute-start.5 = (f32[1,3,256]{2,1,0:T(4,128)S(1)}, f32[1,3,256]{2,1,0:T(4,128)S(1)}, u32[]{:S(2)}, u32[]{:S(2)}) collective-permute-start(f32[1,3,256]{2,1,0:T(4,128)S(1)} %broadcast_select_fusion.7), channel_id=1, source_target_pairs={{0,1},{1,2},{2,3},{3,4},{4,5},{5,6},{6,7},{7,0},{8,9},{9,10},{10,1... | collective-permute-start | bytes 9224 | tf_op jit(solution)/shard_map/while/body/eval_jaxpr/ppermute | solution.py:14
  58.8 5.0 %collective-permute-start.3 = (f32[1,3,256]{2,1,0:T(4,128)S(1)}, f32[1,3,256]{2,1,0:T(4,128)S(1)}, u32[]{:S(2)}, u32[]{:S(2)}) collective-permute-start(f32[1,3,256]{2,1,0:T(4,128)S(1)} %get-tuple-element.1075), channel_id=1, source_target_pairs={{0,1},{1,2},{2,3},{3,4},{4,5},{5,6},{6,7},{7,0},{8,9},{9,10},{10,1... | collective-permute-start | bytes 9224 | tf_op jit(solution)/shard_map/while/body/eval_jaxpr/ppermute | solution.py:14
  59.0 6.2 %collective-permute-start.5 = (f32[1,3,256]{2,1,0:T(4,128)S(1)}, f32[1,3,256]{2,1,0:T(4,128)S(1)}, u32[]{:S(2)}, u32[]{:S(2)}) collective-permute-start(f32[1,3,256]{2,1,0:T(4,128)S(1)} %broadcast_select_fusion.7), channel_id=1, source_target_pairs={{0,1},{1,2},{2,3},{3,4},{4,5},{5,6},{6,7},{7,0},{8,9},{9,10},{10,1... | collective-permute-start | bytes 9224 | tf_op jit(solution)/shard_map/while/body/eval_jaxpr/ppermute | solution.py:14
  65.6 5.0 %collective-permute-start.3 = (f32[1,3,256]{2,1,0:T(4,128)S(1)}, f32[1,3,256]{2,1,0:T(4,128)S(1)}, u32[]{:S(2)}, u32[]{:S(2)}) collective-permute-start(f32[1,3,256]{2,1,0:T(4,128)S(1)} %get-tuple-element.1075), channel_id=1, source_target_pairs={{0,1},{1,2},{2,3},{3,4},{4,5},{5,6},{6,7},{7,0},{8,9},{9,10},{10,1... | collective-permute-start | bytes 9224 | tf_op jit(solution)/shard_map/while/body/eval_jaxpr/ppermute | solution.py:14
  65.7 6.2 %collective-permute-start.5 = (f32[1,3,256]{2,1,0:T(4,128)S(1)}, f32[1,3,256]{2,1,0:T(4,128)S(1)}, u32[]{:S(2)}, u32[]{:S(2)}) collective-permute-start(f32[1,3,256]{2,1,0:T(4,128)S(1)} %broadcast_select_fusion.7), channel_id=1, source_target_pairs={{0,1},{1,2},{2,3},{3,4},{4,5},{5,6},{6,7},{7,0},{8,9},{9,10},{10,1... | collective-permute-start | bytes 9224 | tf_op jit(solution)/shard_map/while/body/eval_jaxpr/ppermute | solution.py:14
  72.3 10.5 %collective-permute-start.10 = (f32[1,3,256]{2,1,0:T(4,128)S(1)}, f32[1,3,256]{2,1,0:T(4,128)S(1)}, u32[]{:S(2)}, u32[]{:S(2)}) collective-permute-start(f32[1,3,256]{2,1,0:T(4,128)S(1)} %get-tuple-element.553), channel_id=1, source_target_pairs={{0,4},{1,5},{2,6},{3,7},{4,0},{5,1},{6,2},{7,3},{8,12},{9,13},{10,... | collective-permute-start | bytes 9224 | tf_op jit(solution)/shard_map/ppermute | solution.py:14
  83.9 5.0 %collective-permute-start.6 = (f32[1,3,256]{2,1,0:T(4,128)S(1)}, f32[1,3,256]{2,1,0:T(4,128)S(1)}, u32[]{:S(2)}, u32[]{:S(2)}) collective-permute-start(f32[1,3,256]{2,1,0:T(4,128)S(1)} %get-tuple-element.1114), channel_id=1, source_target_pairs={{0,1},{1,2},{2,3},{3,4},{4,5},{5,6},{6,7},{7,0},{8,9},{9,10},{10,1... | collective-permute-start | bytes 9224 | tf_op jit(solution)/shard_map/while/body/eval_jaxpr/ppermute | solution.py:14
  85.2 5.0 %collective-permute-start.8 = (f32[1,3,256]{2,1,0:T(4,128)S(1)}, f32[1,3,256]{2,1,0:T(4,128)S(1)}, u32[]{:S(2)}, u32[]{:S(2)}) collective-permute-start(f32[1,3,256]{2,1,0:T(4,128)S(1)} %broadcast_select_fusion.8), channel_id=1, source_target_pairs={{0,1},{1,2},{2,3},{3,4},{4,5},{5,6},{6,7},{7,0},{8,9},{9,10},{10,1... | collective-permute-start | bytes 9224 | tf_op jit(solution)/shard_map/while/body/eval_jaxpr/ppermute | solution.py:14
  90.6 5.0 %collective-permute-start.6 = (f32[1,3,256]{2,1,0:T(4,128)S(1)}, f32[1,3,256]{2,1,0:T(4,128)S(1)}, u32[]{:S(2)}, u32[]{:S(2)}) collective-permute-start(f32[1,3,256]{2,1,0:T(4,128)S(1)} %get-tuple-element.1114), channel_id=1, source_target_pairs={{0,1},{1,2},{2,3},{3,4},{4,5},{5,6},{6,7},{7,0},{8,9},{9,10},{10,1... | collective-permute-start | bytes 9224 | tf_op jit(solution)/shard_map/while/body/eval_jaxpr/ppermute | solution.py:14
  91.1 5.9 %collective-permute-start.8 = (f32[1,3,256]{2,1,0:T(4,128)S(1)}, f32[1,3,256]{2,1,0:T(4,128)S(1)}, u32[]{:S(2)}, u32[]{:S(2)}) collective-permute-start(f32[1,3,256]{2,1,0:T(4,128)S(1)} %broadcast_select_fusion.8), channel_id=1, source_target_pairs={{0,1},{1,2},{2,3},{3,4},{4,5},{5,6},{6,7},{7,0},{8,9},{9,10},{10,1... | collective-permute-start | bytes 9224 | tf_op jit(solution)/shard_map/while/body/eval_jaxpr/ppermute | solution.py:14
  97.4 5.0 %collective-permute-start.6 = (f32[1,3,256]{2,1,0:T(4,128)S(1)}, f32[1,3,256]{2,1,0:T(4,128)S(1)}, u32[]{:S(2)}, u32[]{:S(2)}) collective-permute-start(f32[1,3,256]{2,1,0:T(4,128)S(1)} %get-tuple-element.1114), channel_id=1, source_target_pairs={{0,1},{1,2},{2,3},{3,4},{4,5},{5,6},{6,7},{7,0},{8,9},{9,10},{10,1... | collective-permute-start | bytes 9224 | tf_op jit(solution)/shard_map/while/body/eval_jaxpr/ppermute | solution.py:14
  97.5 6.2 %collective-permute-start.8 = (f32[1,3,256]{2,1,0:T(4,128)S(1)}, f32[1,3,256]{2,1,0:T(4,128)S(1)}, u32[]{:S(2)}, u32[]{:S(2)}) collective-permute-start(f32[1,3,256]{2,1,0:T(4,128)S(1)} %broadcast_select_fusion.8), channel_id=1, source_target_pairs={{0,1},{1,2},{2,3},{3,4},{4,5},{5,6},{6,7},{7,0},{8,9},{9,10},{10,1... | collective-permute-start | bytes 9224 | tf_op jit(solution)/shard_map/while/body/eval_jaxpr/ppermute | solution.py:14
  104.1 5.0 %collective-permute-start.6 = (f32[1,3,256]{2,1,0:T(4,128)S(1)}, f32[1,3,256]{2,1,0:T(4,128)S(1)}, u32[]{:S(2)}, u32[]{:S(2)}) collective-permute-start(f32[1,3,256]{2,1,0:T(4,128)S(1)} %get-tuple-element.1114), channel_id=1, source_target_pairs={{0,1},{1,2},{2,3},{3,4},{4,5},{5,6},{6,7},{7,0},{8,9},{9,10},{10,1... | collective-permute-start | bytes 9224 | tf_op jit(solution)/shard_map/while/body/eval_jaxpr/ppermute | solution.py:14
  104.3 6.2 %collective-permute-start.8 = (f32[1,3,256]{2,1,0:T(4,128)S(1)}, f32[1,3,256]{2,1,0:T(4,128)S(1)}, u32[]{:S(2)}, u32[]{:S(2)}) collective-permute-start(f32[1,3,256]{2,1,0:T(4,128)S(1)} %broadcast_select_fusion.8), channel_id=1, source_target_pairs={{0,1},{1,2},{2,3},{3,4},{4,5},{5,6},{6,7},{7,0},{8,9},{9,10},{10,1... | collective-permute-start | bytes 9224 | tf_op jit(solution)/shard_map/while/body/eval_jaxpr/ppermute | solution.py:14
  110.9 21.7 %collective-permute-start.11 = (f32[1,3,256]{2,1,0:T(4,128)S(1)}, f32[1,3,256]{2,1,0:T(4,128)S(1)}, u32[]{:S(2)}, u32[]{:S(2)}) collective-permute-start(f32[1,3,256]{2,1,0:T(4,128)S(1)} %get-tuple-element.555), channel_id=1, source_target_pairs={{0,4},{1,5},{2,6},{3,7},{4,0},{5,1},{6,2},{7,3},{8,12},{9,13},{10,... | collective-permute-start | bytes 9224 | tf_op jit(solution)/shard_map/ppermute | solution.py:14
  (13 other events, 45.2 us)
where the time goes:
time: 134 us; the launch traced here: 133 us
  waiting for transfers between devices  53 us (40%)
  matrix products  33.7 us (25%)
  blocking collectives  25.8 us (19%)
  local copies, waits for them, and re-layouts  9.09 us (7%)
  starting transfers between devices  7.48 us (6%)
  loops' own time  3.02 us (2%)
    ppermute x39, waiting for transfers between devices, passed_along(): return lax.ppermute(value, axis, pairs)  53 us
    all_gather x2, blocking collectives, entering(): pieces = jax.tree.map(lambda part: lax.all_gather(part, axis), value)  15.4 us
    unnamed x1, blocking collectives  10.4 us
    dot_general x15, matrix products, attract(): jnp.einsum('nij,ncj->nci', kernel, weighted, precision=lax.Precision.HIGH...  10.2 us
    dot_general x15, matrix products, attract(): jnp.einsum('nij,nj->ni', kernel, remote_mass[:, 0], precision=lax.Precisi...  9.77 us
    ppermute x39, starting transfers between devices, passed_along(): return lax.ppermute(value, axis, pairs)  7.48 us
    dot_general x12, matrix products, reaction(): jnp.einsum('nij,ni->nj', kernel, local_mass[:, 0], precision=lax.Precisio...  7.17 us
    dot_general x12, matrix products, reaction(): jnp.einsum('nij,nci->ncj', kernel, weighted, precision=lax.Precision.HIGH...  6.48 us
  transfers between devices with their start and end apart: 39, of which 12 were waited for; matrix products, arithmetic and copies ran while one was open for 24% of the time, Pallas kernels for 0%

commit v1 on v0

v1 whole, which is shorter than its diff:
```python
import functools
import jax
import jax.numpy as jnp
from jax import lax
from jax.experimental import pallas as pl
from jax.experimental.pallas import tpu as pltpu
from jax.sharding import PartitionSpec as P

soften = 0.01
slice_length = 0.25
lobatto_weights = ((5.0 / 24.0, 1.0 / 3.0, -1.0 / 24.0), (-1.0 / 24.0, 1.0 / 3.0, 5.0 / 24.0))
LANES = 128
MESH = pl.DeviceIdType.MESH
EARLY = 4


def round_up(value, step):
    return (value + step - 1) // step * step


def target_of(me, step, count):
    if count & (count - 1) == 0:
        peer, bit = 0, 1
        while bit < count:
            peer = peer + ((me // bit + step // bit) % 2) * bit
            bit *= 2
        return peer
    return (me + step) % count


def source_of(me, step, count):
    if count & (count - 1) == 0:
        return target_of(me, step, count)
    return (me + count - step) % count


def kernel(
    n, slices, body_count, chunk,
    pos, vel, mass, place0, speed0,
    places_out, speeds_out, force_out, start_out, start_speed_out,
    old, first, last, drift, speeds, own, wide, total, force_rows,
    send_old, recv_old, send_first, recv_first, send_last, recv_last, send_drift, recv_drift,
):
    me = lax.axis_index("space")
    slot = lax.axis_index("tm")
    block = pos.shape[3]
    halves = block // LANES
    rows = 3 * halves
    tile = old.shape[1] // 3

    barrier = pltpu.get_barrier_semaphore()
    for step in range(1, n):
        pl.semaphore_signal(barrier, inc=1, device_id={"space": target_of(me, step, n)}, device_id_type=MESH)
    for step in range(1, slices):
        pl.semaphore_signal(barrier, inc=1, device_id={"tm": (slot + step) % slices}, device_id_type=MESH)

    def lanes_of(half):
        return pl.ds(half * LANES, LANES)

    for comp in range(3):
        for half in range(halves):
            row = comp * halves + half
            for node in range(3):
                old[me, pl.ds(node * tile + row, 1), :] = pos[0, node, pl.ds(comp, 1), lanes_of(half)]
                speeds[node, pl.ds(row, 1), :] = vel[0, node, pl.ds(comp, 1), lanes_of(half)]
            own[0, pl.ds(row, 1), :] = place0[pl.ds(comp, 1), lanes_of(half)]
            own[1, pl.ds(row, 1), :] = speed0[pl.ds(comp, 1), lanes_of(half)]
    for half in range(halves):
        old[me, pl.ds(rows + half, 1), :] = mass[:, lanes_of(half)]

    speed = [speeds[node, pl.ds(0, rows), :] for node in range(3)]
    x0 = old[me, pl.ds(0, rows), :]
    half_step = 0.5 * slice_length

    def moved(weights):
        return slice_length * (weights[0] * speed[0] + weights[1] * speed[1] + weights[2] * speed[2])

    x1 = x0 + half_step * (speed[0] - speed[0]) + moved(lobatto_weights[0])
    first[me, pl.ds(0, rows), :] = x1

    def widen(node, ref, offset):
        for comp in range(3):
            for half in range(halves):
                line = ref[me, pl.ds(offset + comp * halves + half, 1), :]
                wide[node, comp, lanes_of(half), :] = jnp.broadcast_to(line, (LANES, LANES)).T

    def copy(ref, send, recv, step):
        return pltpu.make_async_remote_copy(
            src_ref=ref.at[me], dst_ref=ref.at[me], send_sem=send.at[step], recv_sem=recv.at[step],
            device_id={"space": target_of(me, step, n)}, device_id_type=MESH,
        )

    def arrival(ref, send, recv, step):
        whose = source_of(me, step, n)
        pltpu.make_async_remote_copy(
            src_ref=ref.at[whose], dst_ref=ref.at[whose], send_sem=send.at[step], recv_sem=recv.at[step],
            device_id={"space": target_of(me, step, n)}, device_id_type=MESH,
        ).wait_recv()
        return whose

    def pairs(whose, parts, fresh):
        def one_chunk(index, carry):
            span = pl.ds(pl.multiple_of(index * chunk, chunk), chunk)
            for node, ref, offset in parts:
                here = [wide[node, comp, span, :] for comp in range(3)]
                sums = [None] * 3 if fresh else [total[node, comp, span, :] for comp in range(3)]
                for half in range(halves):
                    gap = [ref[whose, pl.ds(offset + comp * halves + half, 1), :] - here[comp] for comp in range(3)]
                    weight = old[whose, pl.ds(rows + half, 1), :]
                    squared = gap[0] * gap[0] + gap[1] * gap[1] + gap[2] * gap[2]
                    inverse = lax.rsqrt(squared + soften)
                    pull = (inverse * inverse) * (inverse * weight)
                    sums = [pull * gap[comp] if sums[comp] is None else sums[comp] + pull * gap[comp] for comp in range(3)]
                for comp in range(3):
                    total[node, comp, span, :] = sums[comp]
            return carry

        lax.fori_loop(0, block // chunk, one_chunk, 0)

    ones = jnp.ones((8, 2 * LANES), jnp.bfloat16)

    def finish(node):
        sums = total[node].reshape(3 * block, LANES)
        high = sums.astype(jnp.bfloat16)
        low = (sums - high.astype(jnp.float32)).astype(jnp.bfloat16)
        both = jnp.concatenate([high, low], axis=1)
        line = lax.dot_general(ones, both, (((1,), (1,)), ((), ())), preferred_element_type=jnp.float32)
        for row in range(rows):
            force_rows[node, pl.ds(row, 1), :] = line[0:1, row * LANES:(row + 1) * LANES]
        return force_rows[node, pl.ds(0, rows), :] / body_count

    old_parts = [(node, old, node * tile) for node in range(3)]
    first_part = [(3, first, 0)]
    last_part = [(4, last, 0)]

    for node in range(3):
        widen(node, old, node * tile)
    pl.semaphore_wait(barrier, n - 1 + slices - 1)
    for step in range(1, n):
        copy(old, send_old, recv_old, step).start()
    for step in range(1, n):
        copy(first, send_first, recv_first, step).start()
    pairs(me, old_parts, True)
    widen(3, first, 0)
    pairs(me, first_part, True)

    def with_first(step, carry):
        whose = arrival(old, send_old, recv_old, step)
        pairs(whose, old_parts, False)
        return carry

    lax.fori_loop(1, n, with_first, 0)

    a_old = [finish(node) for node in range(3)]

    def kicked(weights):
        return slice_length * (weights[0] * a_old[0] + weights[1] * a_old[1] + weights[2] * a_old[2])

    v0, a0 = speed[0], a_old[0]
    v1 = v0 + half_step * (a0 - a_old[0]) + kicked(lobatto_weights[0])
    x2 = x1 + half_step * (v1 - speed[1]) + moved(lobatto_weights[1])
    last[me, pl.ds(0, rows), :] = x2
    for step in range(1, n):
        copy(last, send_last, recv_last, step).start()

    def only_first(step, carry):
        whose = arrival(first, send_first, recv_first, step)
        pairs(whose, first_part, False)
        return carry

    lax.fori_loop(1, n, only_first, 0)
    a1 = finish(3)
    v2 = v1 + half_step * (a1 - a_old[1]) + kicked(lobatto_weights[1])
    drift_rows = drift.shape[1] // 2
    drift[slot, pl.ds(0, rows), :] = x2 - (x0 + slice_length * v0)
    drift[slot, pl.ds(drift_rows, rows), :] = v2 - v0

    def drift_copy(step, whose, to):
        return pltpu.make_async_remote_copy(
            src_ref=drift.at[whose], dst_ref=drift.at[whose], send_sem=send_drift.at[step], recv_sem=recv_drift.at[step],
            device_id={"tm": to}, device_id_type=MESH,
        )

    for step in range(1, slices):
        drift_copy(step, slot, (slot + step) % slices).start()

    widen(4, last, 0)
    pairs(me, last_part, True)

    def put(ref, lead, value):
        for comp in range(3):
            for half in range(halves):
                row = comp * halves + half
                ref[lead + (pl.ds(comp, 1), lanes_of(half))] = value[row:row + 1, :]

    put(places_out, (0, 0), x1)
    put(places_out, (0, 1), x2)
    put(speeds_out, (0, 0), v1)
    put(speeds_out, (0, 1), v2)

    def only_last(step, carry):
        whose = arrival(last, send_last, recv_last, step)
        pairs(whose, last_part, False)
        return carry

    lax.fori_loop(1, n, only_last, 0)
    a2 = finish(4)
    put(force_out, (0,), a2)

    start_place = own[0, pl.ds(0, rows), :] + slot.astype(jnp.float32) * slice_length * own[1, pl.ds(0, rows), :]
    start_speed = own[1, pl.ds(0, rows), :]
    for step in range(1, slices):
        whose = (slot + slices - step) % slices
        drift_copy(step, whose, whose).wait_recv()
        moved_place = drift[whose, pl.ds(0, rows), :]
        moved_speed = drift[whose, pl.ds(drift_rows, rows), :]
        ahead = (slot - 1 - whose).astype(jnp.float32) * slice_length
        counts = whose < slot
        start_place = start_place + jnp.where(counts, moved_place + ahead * moved_speed, 0.0)
        start_speed = start_speed + jnp.where(counts, moved_speed, 0.0)
    put(start_out, (0,), start_place)
    put(start_speed_out, (0,), start_speed)

    for step in range(1, n):
        copy(old, send_old, recv_old, step).wait_send()
        copy(first, send_first, recv_first, step).wait_send()
        copy(last, send_last, recv_last, step).wait_send()
    for step in range(1, slices):
        drift_copy(step, slot, (slot + step) % slices).wait_send()


def solution(mesh):
    n, slices = mesh.shape["space"], mesh.shape["tm"]

    def body(positions, velocities, masses, initial_places, initial_speeds):
        block = positions.shape[3]
        halves = block // LANES
        tile = round_up(4 * halves, 8)
        part = round_up(3 * halves, 8)
        f32 = jnp.float32
        vmem = pl.BlockSpec(memory_space=pltpu.VMEM)
        dma = pltpu.SemaphoreType.DMA
        return pl.pallas_call(
            functools.partial(kernel, n, slices, float(block * n), 64),
            out_shape=(
                jax.ShapeDtypeStruct((1, 2, 3, block), f32),
                jax.ShapeDtypeStruct((1, 2, 3, block), f32),
                jax.ShapeDtypeStruct((1, 3, block), f32),
                jax.ShapeDtypeStruct((1, 3, block), f32),
                jax.ShapeDtypeStruct((1, 3, block), f32),
            ),
            in_specs=[vmem] * 5,
            out_specs=(vmem,) * 5,
            scratch_shapes=[
                pltpu.VMEM((n, 3 * tile, LANES), f32),
                pltpu.VMEM((n, part, LANES), f32),
                pltpu.VMEM((n, part, LANES), f32),
                pltpu.VMEM((slices, 2 * part, LANES), f32),
                pltpu.VMEM((3, part, LANES), f32),
                pltpu.VMEM((2, part, LANES), f32),
                pltpu.VMEM((5, 3, block, LANES), f32),
                pltpu.VMEM((5, 3, block, LANES), f32),
                pltpu.VMEM((5, part, LANES), f32),
                dma((n,)), dma((n,)), dma((n,)), dma((n,)), dma((n,)), dma((n,)),
                dma((slices,)), dma((slices,)),
            ],
            compiler_params=pltpu.CompilerParams(collective_id=0, has_side_effects=True),
        )(positions, velocities, masses.reshape(1, block), initial_places, initial_speeds)

    return jax.shard_map(
        body,
        mesh=mesh,
        in_specs=(
            P("tm", None, None, "space"),
            P("tm", None, None, "space"),
            P("space"),
            P(None, "space"),
            P(None, "space"),
        ),
        out_specs=(
            P("tm", None, None, "space"),
            P("tm", None, None, "space"),
            P("tm", None, "space"),
            P("tm", None, "space"),
            P("tm", None, "space"),
        ),
        check_vma=False,
    )
```

time: 134 us -> 25.8 us (0.19)
  waiting for transfers between devices: 53 us -> 0 us
  matrix products: 33.7 us -> 0 us
  blocking collectives: 25.8 us -> 0 us
  Pallas kernels: 0 us -> 19.1 us
  starting transfers between devices: 7.48 us -> 0 us
  local copies, waits for them, and re-layouts: 9.09 us -> 5.63 us
  loops' own time: 3.02 us -> 0 us
    ppermute x39 -> x0, waiting for transfers between devices: 53 us -> none  [passed_along(): return lax.ppermute(value, axis, pairs)]
    dot_general x54 -> x0, matrix products: 33.7 us -> none  [the longest x15 10.2 us: attract(): jnp.einsum('nij,ncj->nci', kernel, weighted, precision=lax.Precision.HIGH...]
    pallas_call x0 -> x1, Pallas kernels: none -> 19.1 us  [body(): pl.pallas_call(functools.partial(kernel, n, slices, float(block * n), 64)...]
    all_gather x2 -> x0, blocking collectives: 15.4 us -> none  [entering(): pieces = jax.tree.map(lambda part: lax.all_gather(part, axis), value)]
    unnamed x1 -> x0, blocking collectives: 10.4 us -> none
    ppermute x39 -> x0, starting transfers between devices: 7.48 us -> none  [passed_along(): return lax.ppermute(value, axis, pairs)]
    unnamed x26 -> x14, local copies, waits for them, and re-layouts: 5.86 us -> 2.69 us
    another operation x4 -> x0, loops' own time: 3.02 us -> none  [the longest x1 2.02 us: entering(): return lax.fori_loop(0, count - 1, step, so_far)]
  transfers between devices with their start and end apart: 39 -> 0, of which waited for: 12 -> 0; matrix products, arithmetic and copies ran while one was open for 24% -> 0% of each run, Pallas kernels for 0% -> 0%
where the time goes in v1:
time: 25.8 us; the launch traced here: 25.4 us
  Pallas kernels  19.1 us (74%)
  local copies, waits for them, and re-layouts  5.63 us (22%)
  between operations  0.66 us (3%)
    pallas_call x1, Pallas kernels, body(): pl.pallas_call(functools.partial(kernel, n, slices, float(block * n), 64)...  19.1 us
    pallas_call x5, local copies, waits for them, and re-layouts, body(): pl.pallas_call(functools.partial(kernel, n, slices, float(block * n), 64)...  2.94 us
    unnamed x14, local copies, waits for them, and re-layouts  2.69 us

profile of v1, /device:TPU:0, one launch (start us, length us, event | category | flops | bytes accessed | tf_op | source)
XLA Modules:
  0.0 25.4 jit_solution(11458400442342912883)
XLA Ops:
  0.6 0.0 copy-start
  0.6 1.3 %copy.10.pos = f32[1,3,3,256]{3,2,1,0:T(4,128)} copy(f32[1,3,3,256]{3,0,2,1:T(1,128)} %param.5) | data formatting | bytes 18432 | tf_op args[0]
  2.0 0.0 copy-done
  2.0 0.6 %copy.11.vel = f32[1,3,3,256]{3,2,1,0:T(4,128)} copy(f32[1,3,3,256]{3,0,2,1:T(1,128)S(1)} %copy-done) | data formatting | bytes 18432 | tf_op args[1]
  2.6 19.1 %shard_map.92 = (f32[1,2,3,256]{3,2,1,0:T(4,128)}, f32[1,2,3,256]{3,2,1,0:T(4,128)}, f32[1,3,256]{2,1,0:T(4,128)}, f32[1,3,256]{2,1,0:T(4,128)}, f32[1,3,256]{2,1,0:T(4,128)}) custom-call(f32[1,3,3,256]{3,2,1,0:T(4,128)} %copy.10.pos, f32[1,3,3,256]{3,2,1,0:T(4,128)} %copy.11.vel, f32[1,256]{1,0:T(1,128)} %bitcast.1, f32[3,256]{1,0:T(4,128)} %place0.1, ...), custom_call_target="tpu_custom_call" | custom-call | tf_op jit(solution)/shard_map/pallas_call | solution.py:243
  21.7 0.0 copy-start.2
  21.7 0.7 %copy-done.2 = f32[1,2,3,256]{3,2,1,0:T(4,128)S(1)} copy-done((f32[1,2,3,256]{3,2,1,0:T(4,128)S(1)}, f32[1,2,3,256]{3,2,1,0:T(4,128)}, u32[]{:S(2)}) %copy-start.2) | copy-done | bytes 6168
  22.4 0.0 copy-start.5
  22.4 0.0 copy-start.4
  22.4 0.6 %copy.12 = f32[1,2,3,256]{3,1,2,0:T(2,128)} copy(f32[1,2,3,256]{3,2,1,0:T(4,128)S(1)} %copy-done.2) | data formatting | bytes 12288 | tf_op jit(solution)/shard_map/pallas_call | solution.py:243
  23.0 0.1 copy-done.5
  23.0 0.0 copy-start.3
  23.0 0.6 %copy.14 = f32[1,3,256]{2,0,1:T(1,128)} copy(f32[1,3,256]{2,1,0:T(4,128)S(1)} %copy-done.5) | data formatting | bytes 6144 | tf_op jit(solution)/shard_map/pallas_call | solution.py:243
  23.6 0.0 copy-done.4
  23.6 0.0 copy-start.1
  23.6 0.6 %copy.15 = f32[1,3,256]{2,0,1:T(1,128)} copy(f32[1,3,256]{2,1,0:T(4,128)S(1)} %copy-done.4) | data formatting | bytes 6144 | tf_op jit(solution)/shard_map/pallas_call | solution.py:243
  24.2 0.0 copy-done.3
  24.2 0.6 %copy.16 = f32[1,3,256]{2,0,1:T(1,128)} copy(f32[1,3,256]{2,1,0:T(4,128)S(1)} %copy-done.3) | data formatting | bytes 6144 | tf_op jit(solution)/shard_map/pallas_call | solution.py:243
  24.8 0.0 copy-done.1
  24.8 0.6 %copy.13 = f32[1,2,3,256]{3,1,2,0:T(2,128)} copy(f32[1,2,3,256]{3,2,1,0:T(4,128)S(1)} %copy-done.1) | data formatting | bytes 12288 | tf_op jit(solution)/shard_map/pallas_call | solution.py:243
Async XLA Ops:
  0.6 1.3 %copy-start = (f32[1,3,3,256]{3,0,2,1:T(1,128)S(1)}, f32[1,3,3,256]{3,0,2,1:T(1,128)}, u32[]{:S(2)}) copy-start(f32[1,3,3,256]{3,0,2,1:T(1,128)} %param.6) | copy-start | bytes 27652
  21.7 0.7 %copy-start.2 = (f32[1,2,3,256]{3,2,1,0:T(4,128)S(1)}, f32[1,2,3,256]{3,2,1,0:T(4,128)}, u32[]{:S(2)}) copy-start(f32[1,2,3,256]{3,2,1,0:T(4,128)} %get-tuple-element.5) | copy-start | bytes 18436
  22.4 0.7 %copy-start.5 = (f32[1,3,256]{2,1,0:T(4,128)S(1)}, f32[1,3,256]{2,1,0:T(4,128)}, u32[]{:S(2)}) copy-start(f32[1,3,256]{2,1,0:T(4,128)} %get-tuple-element.7) | copy-start | bytes 9220
  22.4 1.3 %copy-start.4 = (f32[1,3,256]{2,1,0:T(4,128)S(1)}, f32[1,3,256]{2,1,0:T(4,128)}, u32[]{:S(2)}) copy-start(f32[1,3,256]{2,1,0:T(4,128)} %get-tuple-element.8) | copy-start | bytes 9220
  23.0 1.2 %copy-start.3 = (f32[1,3,256]{2,1,0:T(4,128)S(1)}, f32[1,3,256]{2,1,0:T(4,128)}, u32[]{:S(2)}) copy-start(f32[1,3,256]{2,1,0:T(4,128)} %get-tuple-element.9) | copy-start | bytes 9220
  23.6 1.2 %copy-start.1 = (f32[1,2,3,256]{3,2,1,0:T(4,128)S(1)}, f32[1,2,3,256]{3,2,1,0:T(4,128)}, u32[]{:S(2)}) copy-start(f32[1,2,3,256]{3,2,1,0:T(4,128)} %get-tuple-element.6) | copy-start | bytes 18436

commit v2 on v1

--- a/solution.py
+++ b/solution.py
@@ -38,13 +38,13 @@
     n, slices, body_count, chunk,
     pos, vel, mass, place0, speed0,
     places_out, speeds_out, force_out, start_out, start_speed_out,
-    old, first, last, drift, speeds, own, wide, total, force_rows,
+    old, first, last, drift, speeds, own, load_sem, wide, total, force_rows,
     send_old, recv_old, send_first, recv_first, send_last, recv_last, send_drift, recv_drift,
 ):
     me = lax.axis_index("space")
     slot = lax.axis_index("tm")
-    block = pos.shape[3]
-    halves = block // LANES
+    halves = mass.shape[0]
+    block = halves * LANES
     rows = 3 * halves
     tile = old.shape[1] // 3
 
@@ -57,16 +57,19 @@
     def lanes_of(half):
         return pl.ds(half * LANES, LANES)
 
-    for comp in range(3):
-        for half in range(halves):
-            row = comp * halves + half
-            for node in range(3):
-                old[me, pl.ds(node * tile + row, 1), :] = pos[0, node, pl.ds(comp, 1), lanes_of(half)]
-                speeds[node, pl.ds(row, 1), :] = vel[0, node, pl.ds(comp, 1), lanes_of(half)]
-            own[0, pl.ds(row, 1), :] = place0[pl.ds(comp, 1), lanes_of(half)]
-            own[1, pl.ds(row, 1), :] = speed0[pl.ds(comp, 1), lanes_of(half)]
-    for half in range(halves):
-        old[me, pl.ds(rows + half, 1), :] = mass[:, lanes_of(half)]
+    loads = [
+        pltpu.make_async_copy(mass.at[:, 0, :], old.at[me, pl.ds(rows, halves), :], load_sem.at[0]),
+        pltpu.make_async_copy(place0, own.at[0], load_sem.at[1]),
+        pltpu.make_async_copy(speed0, own.at[1], load_sem.at[2]),
+    ]
+    for node in range(3):
+        span = pl.ds(node * rows, rows)
+        loads.append(pltpu.make_async_copy(pos.at[span, 0, :], old.at[me, pl.ds(node * tile, rows), :], load_sem.at[3 + node]))
+        loads.append(pltpu.make_async_copy(vel.at[span, 0, :], speeds.at[node, pl.ds(0, rows), :], load_sem.at[6 + node]))
+    for load in loads:
+        load.start()
+    for load in loads:
+        load.wait()
 
     speed = [speeds[node, pl.ds(0, rows), :] for node in range(3)]
     x0 = old[me, pl.ds(0, rows), :]
@@ -187,16 +190,19 @@
     widen(4, last, 0)
     pairs(me, last_part, True)
 
-    def put(ref, lead, value):
+    def put(ref, value):
+        for row in range(rows):
+            ref[row] = value[row:row + 1, :]
+
+    def put_pair(ref, value1, value2):
         for comp in range(3):
             for half in range(halves):
                 row = comp * halves + half
-                ref[lead + (pl.ds(comp, 1), lanes_of(half))] = value[row:row + 1, :]
-
-    put(places_out, (0, 0), x1)
-    put(places_out, (0, 1), x2)
-    put(speeds_out, (0, 0), v1)
-    put(speeds_out, (0, 1), v2)
+                ref[comp, half, 0:1, :] = value1[row:row + 1, :]
+                ref[comp, half, 1:2, :] = value2[row:row + 1, :]
+
+    put_pair(places_out, x1, x2)
+    put_pair(speeds_out, v1, v2)
 
     def only_last(step, carry):
         whose = arrival(last, send_last, recv_last, step)
@@ -205,10 +211,15 @@
 
     lax.fori_loop(1, n, only_last, 0)
     a2 = finish(4)
-    put(force_out, (0,), a2)
-
-    start_place = own[0, pl.ds(0, rows), :] + slot.astype(jnp.float32) * slice_length * own[1, pl.ds(0, rows), :]
-    start_speed = own[1, pl.ds(0, rows), :]
+    put(force_out, a2)
+
+    def in_rows(value):
+        return jnp.concatenate(
+            [value[comp:comp + 1, half * LANES:(half + 1) * LANES] for comp in range(3) for half in range(halves)], axis=0
+        )
+
+    start_speed = in_rows(own[1])
+    start_place = in_rows(own[0]) + slot.astype(jnp.float32) * slice_length * start_speed
     for step in range(1, slices):
         whose = (slot + slices - step) % slices
         drift_copy(step, whose, whose).wait_recv()
@@ -218,8 +229,8 @@
         counts = whose < slot
         start_place = start_place + jnp.where(counts, moved_place + ahead * moved_speed, 0.0)
         start_speed = start_speed + jnp.where(counts, moved_speed, 0.0)
-    put(start_out, (0,), start_place)
-    put(start_speed_out, (0,), start_speed)
+    put(start_out, start_place)
+    put(start_speed_out, start_speed)
 
     for step in range(1, n):
         copy(old, send_old, recv_old, step).wait_send()
@@ -227,6 +238,14 @@
         copy(last, send_last, recv_last, step).wait_send()
     for step in range(1, slices):
         drift_copy(step, slot, (slot + step) % slices).wait_send()
+
+
+def write_out(*refs):
+    copies = [pltpu.make_async_copy(refs[i], refs[5 + i], refs[10].at[i]) for i in range(5)]
+    for copy in copies:
+        copy.start()
+    for copy in copies:
+        copy.wait()
 
 
 def solution(mesh):
@@ -240,16 +259,13 @@
         f32 = jnp.float32
         vmem = pl.BlockSpec(memory_space=pltpu.VMEM)
         dma = pltpu.SemaphoreType.DMA
-        return pl.pallas_call(
+        rows = 3 * halves
+        shapes = [(3, halves, 2, LANES)] * 2 + [(rows, 1, LANES)] * 3
+        anywhere = pl.BlockSpec(memory_space=pl.ANY)
+        outs = pl.pallas_call(
             functools.partial(kernel, n, slices, float(block * n), 64),
-            out_shape=(
-                jax.ShapeDtypeStruct((1, 2, 3, block), f32),
-                jax.ShapeDtypeStruct((1, 2, 3, block), f32),
-                jax.ShapeDtypeStruct((1, 3, block), f32),
-                jax.ShapeDtypeStruct((1, 3, block), f32),
-                jax.ShapeDtypeStruct((1, 3, block), f32),
-            ),
-            in_specs=[vmem] * 5,
+            out_shape=tuple(pltpu.VMEM(shape, f32) for shape in shapes),
+            in_specs=[anywhere] * 5,
             out_specs=(vmem,) * 5,
             scratch_shapes=[
                 pltpu.VMEM((n, 3 * tile, LANES), f32),
@@ -257,7 +273,8 @@
                 pltpu.VMEM((n, part, LANES), f32),
                 pltpu.VMEM((slices, 2 * part, LANES), f32),
                 pltpu.VMEM((3, part, LANES), f32),
-                pltpu.VMEM((2, part, LANES), f32),
+                pltpu.VMEM((2, 3, block), f32),
+                dma((9,)),
                 pltpu.VMEM((5, 3, block, LANES), f32),
                 pltpu.VMEM((5, 3, block, LANES), f32),
                 pltpu.VMEM((5, part, LANES), f32),
@@ -265,7 +282,22 @@
                 dma((slices,)), dma((slices,)),
             ],
             compiler_params=pltpu.CompilerParams(collective_id=0, has_side_effects=True),
-        )(positions, velocities, masses.reshape(1, block), initial_places, initial_speeds)
+        )(
+            positions.reshape(3 * rows, 1, LANES),
+            velocities.reshape(3 * rows, 1, LANES),
+            masses.reshape(halves, 1, LANES),
+            initial_places,
+            initial_speeds,
+        )
+        outs = pl.pallas_call(
+            write_out,
+            out_shape=tuple(jax.ShapeDtypeStruct(shape, f32) for shape in shapes),
+            in_specs=[vmem] * 5,
+            out_specs=(anywhere,) * 5,
+            scratch_shapes=[dma((5,))],
+        )(*(pltpu.with_memory_space_constraint(part, pltpu.VMEM) for part in outs))
+        paired = [part.transpose(2, 0, 1, 3).reshape(1, 2, 3, block) for part in outs[:2]]
+        return (*paired, *(part.reshape(1, 3, block) for part in outs[2:]))
 
     return jax.shard_map(
         body,

time: 25.8 us -> 19.2 us (0.74)
  local copies, waits for them, and re-layouts: 5.63 us -> 0 us
  Pallas kernels: 19.1 us -> 18.4 us
    pallas_call x5 -> x0, local copies, waits for them, and re-layouts: 2.94 us -> none  [body(): pl.pallas_call(functools.partial(kernel, n, slices, float(block * n), 64)...]
    unnamed x14 -> x0, local copies, waits for them, and re-layouts: 2.69 us -> none
    pallas_call x1, Pallas kernels: 19.1 us -> 17.8 us  [body(): pl.pallas_call(functools.partial(kernel, n, slices, float(block * n), 64)...]
    pallas_call x0 -> x1, Pallas kernels: none -> 0.65 us  [body(): pl.pallas_call(write_out, out_shape=tuple((jax.ShapeDtypeStruct(shape, f3...]
where the time goes in v2:
time: 19.2 us; the launch traced here: 19 us
  Pallas kernels  18.4 us (96%)
  between operations  0.64 us (3%)
    pallas_call x1, Pallas kernels, body(): pl.pallas_call(functools.partial(kernel, n, slices, float(block * n), 64)...  17.8 us
    pallas_call x1, Pallas kernels, body(): pl.pallas_call(write_out, out_shape=tuple((jax.ShapeDtypeStruct(shape, f3...  0.65 us

profile of v2, /device:TPU:0, one launch (start us, length us, event | category | flops | bytes accessed | tf_op | source)
XLA Modules:
  0.0 19.0 jit_solution(256098703042080664)
XLA Ops:
  0.6 17.8 %shard_map.92 = (f32[3,2,2,128]{3,2,1,0:T(2,128)S(1)}, f32[3,2,2,128]{3,2,1,0:T(2,128)S(1)}, f32[6,1,128]{2,1,0:T(1,128)S(1)}, f32[6,1,128]{2,1,0:T(1,128)S(1)}, f32[6,1,128]{2,1,0:T(1,128)S(1)}) custom-call(f32[18,1,128]{2,1,0:T(1,128)} %bitcast.12, f32[18,1,128]{2,1,0:T(1,128)} %bitcast.13, f32[2,1,128]{2,1,0:T(1,128)} %bitcast.14, f32[3,256]{1,0:T(4,128)} %place0.1, ...), custom_call_target="tpu_custom_call" | custom-call | tf_op jit(solution)/shard_map/pallas_call | solution.py:265
  18.4 0.7 %shard_map.93 = (f32[3,2,2,128]{3,2,1,0:T(2,128)}, f32[3,2,2,128]{3,2,1,0:T(2,128)}, f32[6,1,128]{2,1,0:T(1,128)}, f32[6,1,128]{2,1,0:T(1,128)}, f32[6,1,128]{2,1,0:T(1,128)}) custom-call(f32[3,2,2,128]{3,2,1,0:T(2,128)S(1)} %get-tuple-element.15.refs_0_, f32[3,2,2,128]{3,2,1,0:T(2,128)S(1)} %get-tuple-element.16.refs_1_, ...), custom_call_target="tpu_custom_call" | custom-call | tf_op jit(solution)/shard_map/pallas_call | solution.py:292

commit v3 on v2

--- a/solution.py
+++ b/solution.py
@@ -46,7 +46,7 @@
     halves = mass.shape[0]
     block = halves * LANES
     rows = 3 * halves
-    tile = old.shape[1] // 3
+    used = {id(old): 3 * rows + halves, id(first): rows, id(last): rows}
 
     barrier = pltpu.get_barrier_semaphore()
     for step in range(1, n):
@@ -58,13 +58,13 @@
         return pl.ds(half * LANES, LANES)
 
     loads = [
-        pltpu.make_async_copy(mass.at[:, 0, :], old.at[me, pl.ds(rows, halves), :], load_sem.at[0]),
+        pltpu.make_async_copy(mass.at[:, 0, :], old.at[me, pl.ds(3 * rows, halves), :], load_sem.at[0]),
         pltpu.make_async_copy(place0, own.at[0], load_sem.at[1]),
         pltpu.make_async_copy(speed0, own.at[1], load_sem.at[2]),
     ]
     for node in range(3):
         span = pl.ds(node * rows, rows)
-        loads.append(pltpu.make_async_copy(pos.at[span, 0, :], old.at[me, pl.ds(node * tile, rows), :], load_sem.at[3 + node]))
+        loads.append(pltpu.make_async_copy(pos.at[span, 0, :], old.at[me, pl.ds(node * rows, rows), :], load_sem.at[3 + node]))
         loads.append(pltpu.make_async_copy(vel.at[span, 0, :], speeds.at[node, pl.ds(0, rows), :], load_sem.at[6 + node]))
     for load in loads:
         load.start()
@@ -89,14 +89,14 @@
 
     def copy(ref, send, recv, step):
         return pltpu.make_async_remote_copy(
-            src_ref=ref.at[me], dst_ref=ref.at[me], send_sem=send.at[step], recv_sem=recv.at[step],
+            src_ref=ref.at[me, pl.ds(0, used[id(ref)]), :], dst_ref=ref.at[me, pl.ds(0, used[id(ref)]), :], send_sem=send.at[step], recv_sem=recv.at[step],
             device_id={"space": target_of(me, step, n)}, device_id_type=MESH,
         )
 
     def arrival(ref, send, recv, step):
         whose = source_of(me, step, n)
         pltpu.make_async_remote_copy(
-            src_ref=ref.at[whose], dst_ref=ref.at[whose], send_sem=send.at[step], recv_sem=recv.at[step],
+            src_ref=ref.at[whose, pl.ds(0, used[id(ref)]), :], dst_ref=ref.at[whose, pl.ds(0, used[id(ref)]), :], send_sem=send.at[step], recv_sem=recv.at[step],
             device_id={"space": target_of(me, step, n)}, device_id_type=MESH,
         ).wait_recv()
         return whose
@@ -109,7 +109,7 @@
                 sums = [None] * 3 if fresh else [total[node, comp, span, :] for comp in range(3)]
                 for half in range(halves):
                     gap = [ref[whose, pl.ds(offset + comp * halves + half, 1), :] - here[comp] for comp in range(3)]
-                    weight = old[whose, pl.ds(rows + half, 1), :]
+                    weight = old[whose, pl.ds(3 * rows + half, 1), :]
                     squared = gap[0] * gap[0] + gap[1] * gap[1] + gap[2] * gap[2]
                     inverse = lax.rsqrt(squared + soften)
                     pull = (inverse * inverse) * (inverse * weight)
@@ -132,17 +132,17 @@
             force_rows[node, pl.ds(row, 1), :] = line[0:1, row * LANES:(row + 1) * LANES]
         return force_rows[node, pl.ds(0, rows), :] / body_count
 
-    old_parts = [(node, old, node * tile) for node in range(3)]
+    old_parts = [(node, old, node * rows) for node in range(3)]
     first_part = [(3, first, 0)]
     last_part = [(4, last, 0)]
 
+    pl.semaphore_wait(barrier, n - 1 + slices - 1)
+    for step in range(1, n):
+        copy(old, send_old, recv_old, step).start()
+    for step in range(1, n):
+        copy(first, send_first, recv_first, step).start()
     for node in range(3):
-        widen(node, old, node * tile)
-    pl.semaphore_wait(barrier, n - 1 + slices - 1)
-    for step in range(1, n):
-        copy(old, send_old, recv_old, step).start()
-    for step in range(1, n):
-        copy(first, send_first, recv_first, step).start()
+        widen(node, old, node * rows)
     pairs(me, old_parts, True)
     widen(3, first, 0)
     pairs(me, first_part, True)
@@ -254,7 +254,7 @@
     def body(positions, velocities, masses, initial_places, initial_speeds):
         block = positions.shape[3]
         halves = block // LANES
-        tile = round_up(4 * halves, 8)
+        packed = round_up(10 * halves, 8)
         part = round_up(3 * halves, 8)
         f32 = jnp.float32
         vmem = pl.BlockSpec(memory_space=pltpu.VMEM)
@@ -268,7 +268,7 @@
             in_specs=[anywhere] * 5,
             out_specs=(vmem,) * 5,
             scratch_shapes=[
-                pltpu.VMEM((n, 3 * tile, LANES), f32),
+                pltpu.VMEM((n, packed, LANES), f32),
                 pltpu.VMEM((n, part, LANES), f32),
                 pltpu.VMEM((n, part, LANES), f32),
                 pltpu.VMEM((slices, 2 * part, LANES), f32),

time: 19.2 us -> 19.2 us (level)
  no operation moved by 1% of the time
where the time goes in v3:
time: 19.2 us; the launch traced here: 19.1 us
  Pallas kernels  18.5 us (96%)
  between operations  0.64 us (3%)
    pallas_call x1, Pallas kernels, body(): pl.pallas_call(functools.partial(kernel, n, slices, float(block * n), 64)...  17.8 us
    pallas_call x1, Pallas kernels, body(): pl.pallas_call(write_out, out_shape=tuple((jax.ShapeDtypeStruct(shape, f3...  0.65 us

profile of v3, /device:TPU:0, one launch (start us, length us, event | category | flops | bytes accessed | tf_op | source)
XLA Modules:
  0.0 19.1 jit_solution(9680499086580480379)
XLA Ops:
  0.6 17.8 %shard_map.92 = (f32[3,2,2,128]{3,2,1,0:T(2,128)S(1)}, f32[3,2,2,128]{3,2,1,0:T(2,128)S(1)}, f32[6,1,128]{2,1,0:T(1,128)S(1)}, f32[6,1,128]{2,1,0:T(1,128)S(1)}, f32[6,1,128]{2,1,0:T(1,128)S(1)}) custom-call(f32[18,1,128]{2,1,0:T(1,128)} %bitcast.12, f32[18,1,128]{2,1,0:T(1,128)} %bitcast.13, f32[2,1,128]{2,1,0:T(1,128)} %bitcast.14, f32[3,256]{1,0:T(4,128)} %place0.1, ...), custom_call_target="tpu_custom_call" | custom-call | tf_op jit(solution)/shard_map/pallas_call | solution.py:265
  18.4 0.7 %shard_map.93 = (f32[3,2,2,128]{3,2,1,0:T(2,128)}, f32[3,2,2,128]{3,2,1,0:T(2,128)}, f32[6,1,128]{2,1,0:T(1,128)}, f32[6,1,128]{2,1,0:T(1,128)}, f32[6,1,128]{2,1,0:T(1,128)}) custom-call(f32[3,2,2,128]{3,2,1,0:T(2,128)S(1)} %get-tuple-element.15.refs_0_, f32[3,2,2,128]{3,2,1,0:T(2,128)S(1)} %get-tuple-element.16.refs_1_, ...), custom_call_target="tpu_custom_call" | custom-call | tf_op jit(solution)/shard_map/pallas_call | solution.py:292
